TPU v7x, 32 devices: a whole 2x2x4 slice. The times are simulated.
32 devices in a mesh: outer: 8 (over z, x), inner: 4 (over y, core).
Axes of the slice: x: 2, y: 2, z: 4, core: 2. Of those that a mesh axis runs over, the one named last changes fastest.
Arguments:
- queries: bfloat16 [8192, 1024], P(('outer', 'inner')), may hold values from -10 to 10
- keys: bfloat16 [8192, 256], P(('outer', 'inner')), may hold values from -10 to 10
- values: bfloat16 [8192, 256], P(('outer', 'inner')), may hold values from -18 to 18
- pool_fine: float32 [16, 8], replicated, may hold values from -1.5 to 1.5
- pool_coarse: float32 [8, 8], replicated, may hold values from -2 to 2
- gain: float32 [1024], replicated, may hold values from 0.5 to 1.5
Outputs:
- normed: bfloat16 [8192, 1024], P(('outer', 'inner'))
All inputs are finite; a program needn't handle non-finite values.
Results may differ from a plain program's by a relative error of at most 0.008.
Values may be sent and summed in bfloat16 or wider, within the bound.
A program may use at most 64 MiB of HBM per device.

v0:
```python
import functools
import math

import jax
import jax.numpy as jnp
from jax import lax
from jax.experimental import pallas as pl
from jax.experimental.pallas import tpu as pltpu
from jax.sharding import PartitionSpec as P

HQ = 16
KVH = 4
HD = 64
BLOCK = 512
FINE = 16
RATIO = 8
COARSE = 128

EPSILON = 1e-06
MASKED_SCORE = -1e30
LANES = 128
MESH = pl.DeviceIdType.MESH
BF16 = jnp.bfloat16
F32 = jnp.float32


def kernel(
    outer_count, inner_count,
    q_hbm, k_hbm, v_hbm, pf_hbm, pc_hbm, out_ref,
    q_ref, k_ref, v_ref, pf_ref, pc_ref, in_sems,
    q_all, own_k, own_v, mate_k, mate_v, other_k, other_v,
    ka, va, kb, vb, kc, vc, bias_ref,
    fine_send, fine_all, coarse_send, coarse_pad, coarse_group, coarse_all,
    peaks, sums, att_send, att_recv,
    q_ss, q_rs, own_ss, own_rs, mate_ss, mate_rs, other_ss, other_rs,
    fine_ss, fine_rs, cg_ss, cg_rs, co_ss, co_rs, att_ss, att_rs,
):
    tok = q_ref.shape[0]
    ranks = BLOCK // tok
    kv_width = KVH * HD
    share = kv_width // ranks
    q_share = HQ * HD // ranks
    tiles = q_share // LANES
    kv_local = share // HD
    tiles_per_kv = tiles // kv_local
    rows_kv = tiles_per_kv * tok
    fine_dev = tok // FINE
    coarse_dev = tok // COARSE
    group_tok = tok * inner_count
    fine_amount = group_tok // FINE
    coarse_amount = outer_count * group_tok // COARSE
    blocks = outer_count * inner_count // ranks
    factor = HD ** (-0.5) * math.log2(math.e)

    o_me = lax.axis_index("outer")
    i_me = lax.axis_index("inner")
    linear = o_me * inner_count + i_me
    block = linear // ranks
    rank = lax.rem(linear, ranks)
    odd = lax.rem(block, 2)
    mate = block + 1 - 2 * odd
    relay_from = block - 2 + 4 * odd
    relay_to = block + 2 - 4 * odd
    has_other = (relay_from >= 0) & (relay_from < blocks)
    has_next = (relay_to >= 0) & (relay_to < blocks)

    def at_rank(which_block, rel):
        target_rank = lax.rem(rank + rel, ranks)
        spot = which_block * ranks + target_rank
        return (spot // inner_count, lax.rem(spot, inner_count)), target_rank

    inner_peers = [lax.rem(i_me + rel, inner_count) for rel in range(1, inner_count)]
    outer_peers = [lax.rem(o_me + rel, outer_count) for rel in range(1, outer_count)]

    loads = [
        pltpu.make_async_copy(src, dst, in_sems.at[n])
        for n, (src, dst) in enumerate((
            (k_hbm, k_ref), (q_hbm, q_ref), (v_hbm, v_ref), (pf_hbm, pf_ref), (pc_hbm, pc_ref)))
    ]
    for load in loads:
        load.start()

    barrier = pltpu.get_barrier_semaphore()

    def greet(device):
        pl.semaphore_signal(barrier, inc=1, device_id=device, device_id_type=MESH)

    for peer in inner_peers:
        greet((o_me, peer))
    for peer in outer_peers:
        greet((peer, i_me))
    for rel in range(ranks):
        greet(at_rank(mate, rel)[0])

    for which in (relay_from, relay_to):
        greet(at_rank(lax.rem(which + blocks, blocks), 0)[0])

    for load in loads:
        load.wait()

    def remote(src, dst, send_sem, recv_sem, device):
        return pltpu.make_async_remote_copy(
            src_ref=src, dst_ref=dst, send_sem=send_sem, recv_sem=recv_sem,
            device_id=device, device_id_type=MESH,
        )

    def cols(index, width):
        return pl.ds(pl.multiple_of(index * width, LANES), width)

    own_copies = []
    for rel in range(1, ranks):
        device, target = at_rank(block, rel)
        slot = ranks - rel
        own_copies.append(remote(
            k_ref.at[:, cols(target, share)], own_k.at[slot],
            own_ss.at[0, slot], own_rs.at[0, slot], device))
        own_copies.append(remote(
            q_ref.at[:, cols(target, q_share)], q_all.at[slot],
            q_ss.at[slot], q_rs.at[slot], device))
        own_copies.append(remote(
            v_ref.at[:, cols(target, share)], own_v.at[slot],
            own_ss.at[1, slot], own_rs.at[1, slot], device))

    def mate_copies_of(part, src, dst):
        made = []
        for rel in range(ranks):
            device, target = at_rank(mate, rel)
            slot = (ranks - rel) % ranks
            made.append(remote(
                src.at[:, cols(target, share)], dst.at[slot],
                mate_ss.at[part, slot], mate_rs.at[part, slot], device))
        return made

    def relay_copies(part):
        device = at_rank(relay_to, 0)[0]
        src, dst = ((mate_k, other_k), (mate_v, other_v))[part]
        return [remote(src.at[slot], dst.at[slot], other_ss.at[part, slot],
                       other_rs.at[part, slot], device) for slot in range(ranks)]

    mate_k_copies = mate_copies_of(0, k_ref, mate_k)
    mate_v_copies = mate_copies_of(1, v_ref, mate_v)

    def spread(pool):
        rows = pool.shape[0]
        return jnp.concatenate(
            [jnp.broadcast_to(pool[:, n:n + 1], (rows, HD)) for n in range(2 * KVH)], axis=1)

    pf = spread(pf_ref[...].T)
    pc = spread(pc_ref[...])
    paired = jnp.concatenate([k_ref[...], v_ref[...]], axis=1).astype(F32)
    fine = jnp.sum(paired.reshape(fine_dev, FINE, 2 * kv_width) * pf[None], axis=1).astype(BF16)
    fine_wide = fine.astype(F32)
    coarse = jnp.sum(
        fine_wide.reshape(coarse_dev, RATIO, 2 * kv_width) * pc[None], axis=1).astype(BF16)
    padded = -(-coarse_dev // 8) * 8
    coarse_wide = coarse.astype(F32)
    if padded > coarse_dev:
        coarse_wide = jnp.concatenate(
            [coarse_wide, jnp.zeros((padded - coarse_dev, 2 * kv_width), F32)], axis=0)
    for n in range(ranks):
        k_cols = slice(n * share, (n + 1) * share)
        v_cols = slice(kv_width + n * share, kv_width + (n + 1) * share)
        fine_send[n] = jnp.concatenate([fine[:, k_cols], fine[:, v_cols]], axis=1)
        coarse_send[n] = jnp.concatenate([coarse_wide[:, k_cols], coarse_wide[:, v_cols]], axis=1)
    fine_all[i_me] = fine_send[rank]
    coarse_pad[i_me] = coarse_send[rank]

    group_copies = []
    for n, peer in enumerate(inner_peers):
        peer_rank = lax.rem(peer, ranks)
        group_copies.append(remote(
            coarse_send.at[peer_rank], coarse_pad.at[i_me],
            cg_ss.at[n], cg_rs.at[n], (o_me, peer)))
        group_copies.append(remote(
            fine_send.at[peer_rank], fine_all.at[i_me],
            fine_ss.at[n], fine_rs.at[n], (o_me, peer)))

    low = (lax.broadcasted_iota(jnp.int32, (1, LANES), 1) < HD).astype(F32).astype(BF16)
    high = (lax.broadcasted_iota(jnp.int32, (1, LANES), 1) >= HD).astype(F32).astype(BF16)

    def variants(k_raw, v_raw, k_out, v_out, rows):
        k_swap = pltpu.roll(k_raw.astype(F32), HD, 1).astype(BF16)
        v_swap = pltpu.roll(v_raw.astype(F32), HD, 1).astype(BF16)
        for n in range(kv_local):
            at_low = (k_raw, v_raw) if n == 0 else (k_swap, v_swap)
            at_high = (k_swap, v_swap) if n == 0 else (k_raw, v_raw)
            k_out[n, 0, rows, :] = at_low[0] * low
            k_out[n, 1, rows, :] = at_high[0] * high
            v_out[n, 0, rows, :] = at_low[1] * low + high
            v_out[n, 1, rows, :] = at_high[1] * high + low

    def unit(part, n, half, k_set, v_set, span, bias, first):
        query = jnp.concatenate(
            [q_all[part, :, cols(n * tiles_per_kv + x, LANES)] for x in range(tiles_per_kv)],
            axis=0)
        scores = lax.dot_general(
            query, k_set[n, half, span, :], (((1,), (1,)), ((), ())),
            preferred_element_type=F32)
        if bias is not None:
            scores = scores + bias
        peak = jnp.broadcast_to(jnp.max(scores, axis=1, keepdims=True), (rows_kv, LANES))
        at = (part * kv_local + n) * 2 + half
        if not first:
            before = peaks[at]
            peak = jnp.maximum(peak, before)
        wide = jnp.concatenate([peak] * (scores.shape[1] // LANES), axis=1)
        weights = jnp.exp2((scores - wide) * factor).astype(BF16)
        blended = jnp.dot(weights, v_set[n, half, span, :], preferred_element_type=F32)
        if not first:
            blended = blended + sums[at] * jnp.exp2((before - peak) * factor)
        return at, peak, blended

    def stage(start, stop, k_set, v_set, span, first):
        def body(step, carry):
            part = start + step // kv_local
            n = lax.rem(step, kv_local)
            for at, peak, blended in [
                unit(part, n, half, k_set, v_set, span, None, first) for half in range(2)
            ]:
                peaks[at] = peak
                sums[at] = blended
            return carry
        lax.fori_loop(0, (stop - start) * kv_local, body, 0)

    q_all[0] = q_ref[:, cols(rank, q_share)]
    variants(k_ref[:, cols(rank, share)], v_ref[:, cols(rank, share)], ka, va, slice(0, tok))
    stage(0, 1, ka, va, slice(0, tok), True)

    pl.semaphore_wait(barrier, inner_count - 1 + outer_count - 1 + ranks + 2)
    for copy in own_copies + mate_k_copies + group_copies + mate_v_copies:
        copy.start()

    for copy in own_copies:
        copy.wait_recv()
    for slot in range(1, ranks):
        variants(own_k[slot], own_v[slot], ka, va, slice(slot * tok, (slot + 1) * tok))
        variants(own_k[slot], own_v[slot], kb, vb, slice((slot - 1) * tok, slot * tok))

    stage(1, ranks, ka, va, slice(0, BLOCK), True)

    for copy in group_copies:
        copy.wait_recv()
    for n in range(inner_count):
        coarse_group[n * coarse_dev:(n + 1) * coarse_dev, :] = coarse_pad[n, 0:coarse_dev, :]
    coarse_all[o_me] = coarse_group[...]
    outer_copies = []
    for n, peer in enumerate(outer_peers):
        outer_copies.append(remote(
            coarse_group, coarse_all.at[o_me], co_ss.at[n], co_rs.at[n], (peer, i_me)))
    for copy in outer_copies:
        copy.start()

    for part, copies in enumerate((mate_k_copies, mate_v_copies)):
        for copy in copies:
            copy.wait_recv()

        @pl.when(has_next)
        def _():
            for copy in relay_copies(part):
                copy.start()
    for slot in range(ranks):
        variants(mate_k[slot], mate_v[slot], kb, vb,
                 slice(BLOCK + (slot - 1) * tok, BLOCK + slot * tok))
    stage(0, 1, kb, vb, slice(0, 2 * BLOCK - tok), False)
    stage(1, ranks, kb, vb, slice(BLOCK - tok, 2 * BLOCK - tok), False)

    for copy in outer_copies:
        copy.wait_recv()
    fine_rows = fine_all[...].reshape(fine_amount, 2 * share)
    variants(fine_rows[:, :share], fine_rows[:, share:], kc, vc, slice(BLOCK, BLOCK + fine_amount))
    coarse_rows = coarse_all[...].reshape(coarse_amount, 2 * share).astype(BF16)
    variants(coarse_rows[:, :share], coarse_rows[:, share:], kc, vc,
             slice(BLOCK + fine_amount, BLOCK + fine_amount + coarse_amount))
    far = fine_amount + coarse_amount
    spot = lax.broadcasted_iota(jnp.int32, (1, far), 1)
    fine_pos = o_me * group_tok + spot * FINE
    coarse_pos = (spot - fine_amount) * COARSE
    position = jnp.where(spot < fine_amount, fine_pos, coarse_pos)
    distance = jnp.abs(lax.div(position, BLOCK) - block)
    outside = (spot < fine_amount) | (lax.div(position, group_tok) != o_me)
    bias_ref[:, BLOCK:] = jnp.where((distance > 1) & outside, 0.0, MASKED_SCORE)

    @pl.when(has_other)
    def _():
        for copy in relay_copies(0) + relay_copies(1):
            copy.wait_recv()
        for slot in range(ranks):
            variants(other_k[slot], other_v[slot], kc, vc, slice(slot * tok, (slot + 1) * tok))
        bias_ref[:, :BLOCK] = jnp.zeros((1, BLOCK), F32)

    @pl.when(jnp.logical_not(has_other))
    def _():
        zero = jnp.zeros((BLOCK, LANES), BF16)
        for n in range(kv_local):
            for half in range(2):
                kc[n, half, 0:BLOCK, :] = zero
                vc[n, half, 0:BLOCK, :] = zero
        bias_ref[:, :BLOCK] = jnp.full((1, BLOCK), MASKED_SCORE, F32)

    is_low = lax.broadcasted_iota(jnp.int32, (1, LANES), 1) < HD

    def finish(part, n):
        lower, upper = [
            unit(part, n, half, kc, vc, slice(None), bias_ref[...], False)[2] for half in range(2)]
        totals = pltpu.roll(jnp.where(is_low, upper, lower), HD, 1)
        return jnp.where(is_low, lower, upper) / totals

    def att_copy(part, tile):
        device, _ = at_rank(block, part)
        slot = ranks - part - 1
        return remote(att_send.at[part - 1, tile], att_recv.at[slot, tile],
                      att_ss.at[slot, tile], att_rs.at[slot, tile], device)

    for part in range(1, ranks):
        def give(n, carry):
            attended = finish(part, n)
            for x in range(tiles_per_kv):
                tile = n * tiles_per_kv + x
                att_send[part - 1, tile] = attended[x * tok:(x + 1) * tok]
                att_copy(part, tile).start()
            return carry
        lax.fori_loop(0, kv_local, give, 0)

    def keep(n, carry):
        attended = finish(0, n)
        for x in range(tiles_per_kv):
            tile = n * tiles_per_kv + x
            out_ref[:, cols(rank * tiles + tile, LANES)] = attended[x * tok:(x + 1) * tok]
        return carry

    lax.fori_loop(0, kv_local, keep, 0)
    for part in range(1, ranks):
        slot = ranks - part
        column = lax.rem(rank + slot, ranks) * tiles
        for tile in range(tiles):
            att_copy(part, tile).wait_recv()
            out_ref[:, cols(column + tile, LANES)] = att_recv[slot - 1, tile]

    for copy in own_copies + mate_k_copies + mate_v_copies + group_copies + outer_copies:
        copy.wait_send()

    @pl.when(has_next)
    def _():
        for copy in relay_copies(0) + relay_copies(1):
            copy.wait_send()

    for part in range(1, ranks):
        for tile in range(tiles):
            att_copy(part, tile).wait_send()


def norm_kernel(attended_ref, gain_ref, out_ref):
    attended = attended_ref[...]
    rescale = lax.rsqrt(jnp.mean(attended * attended, axis=1, keepdims=True) + EPSILON)
    out_ref[...] = (attended * rescale * gain_ref[...]).astype(BF16)


def local(outer_count, inner_count, queries, keys, values, pool_fine, pool_coarse, gain):
    tok = queries.shape[0]
    ranks = BLOCK // tok
    share = KVH * HD // ranks
    kv_local = share // HD
    q_share = HQ * HD // ranks
    tiles = q_share // LANES
    group_tok = tok * inner_count
    far = group_tok // FINE + outer_count * group_tok // COARSE
    coarse_dev = tok // COARSE
    padded = -(-coarse_dev // 8) * 8
    assert ranks >= 2 and BLOCK % tok == 0 and kv_local == 2 and share == LANES
    assert inner_count % ranks == 0 and (outer_count * inner_count // ranks) % 2 == 0
    dma = pltpu.SemaphoreType.DMA
    vmem = pltpu.VMEM
    near = lambda: vmem((ranks, tok, share), BF16)
    sets = lambda amount: vmem((kv_local, 2, amount, LANES), BF16)
    units = ranks * kv_local * 2
    rows_kv = tiles // kv_local * tok
    pair = lambda: dma((2, ranks))
    attended = pl.pallas_call(
        functools.partial(kernel, outer_count, inner_count),
        out_shape=jax.ShapeDtypeStruct((tok, HQ * HD), F32),
        in_specs=[pl.BlockSpec(memory_space=pltpu.HBM)] * 5,
        out_specs=pl.BlockSpec(memory_space=pltpu.VMEM),
        scratch_shapes=[
            vmem(queries.shape, BF16), vmem(keys.shape, BF16), vmem(values.shape, BF16),
            vmem(pool_fine.shape[::-1], F32), vmem(pool_coarse.shape, F32), dma((5,)),
            vmem((ranks, tok, q_share), BF16),
            near(), near(), near(), near(), near(), near(),
            sets(BLOCK), sets(BLOCK), sets(2 * BLOCK - tok), sets(2 * BLOCK - tok),
            sets(BLOCK + far), sets(BLOCK + far), vmem((1, BLOCK + far), F32),
            vmem((ranks, tok // FINE, 2 * share), BF16),
            vmem((inner_count, tok // FINE, 2 * share), BF16),
            vmem((ranks, padded, 2 * share), F32),
            vmem((inner_count, padded, 2 * share), F32),
            vmem((inner_count * coarse_dev, 2 * share), F32),
            vmem((outer_count, inner_count * coarse_dev, 2 * share), F32),
            vmem((units, rows_kv, LANES), F32),
            vmem((units, rows_kv, LANES), F32),
            vmem((ranks - 1, tiles, tok, LANES), F32),
            vmem((ranks - 1, tiles, tok, LANES), F32),
            dma((ranks,)), dma((ranks,)),
            pair(), pair(), pair(), pair(), pair(), pair(),
            dma((inner_count - 1,)), dma((inner_count - 1,)),
            dma((inner_count - 1,)), dma((inner_count - 1,)),
            dma((outer_count - 1,)), dma((outer_count - 1,)),
            dma((ranks - 1, tiles)), dma((ranks - 1, tiles)),
        ],
        compiler_params=pltpu.CompilerParams(
            collective_id=0, has_side_effects=True, vmem_limit_bytes=32 * 1024 * 1024),
    )(*(pltpu.with_memory_space_constraint(array, pltpu.HBM) for array in (
        queries, keys, values, pool_fine.T, pool_coarse)))
    return pl.pallas_call(
        norm_kernel,
        out_shape=jax.ShapeDtypeStruct((tok, HQ * HD), BF16),
        in_specs=[pl.BlockSpec(memory_space=pltpu.VMEM)] * 2,
        out_specs=pl.BlockSpec(memory_space=pltpu.VMEM),
        compiler_params=pltpu.CompilerParams(vmem_limit_bytes=8 * 1024 * 1024),
    )(attended, gain.reshape(1, -1))


def solution(mesh):
    rows = P(("outer", "inner"), None)
    return jax.shard_map(
        functools.partial(local, mesh.shape["outer"], mesh.shape["inner"]),
        mesh=mesh, in_specs=(rows, rows, rows, P(), P(), P()),
        out_specs=rows, check_vma=False,
    )
```

profile of v0, /device:TPU:9, one launch (start us, length us, event | category | flops | bytes accessed | tf_op | source)
XLA Modules:
  0.0 27.7 jit_solution(6863229593478810221)
XLA Ops:
  0.0 0.0 copy-start
  0.0 26.7 %shard_map.64.attended_ref = f32[256,1024]{1,0:T(8,128)S(1)} custom-call(bf16[256,1024]{1,0:T(8,128)(2,1)} %q_hbm.1, bf16[256,256]{1,0:T(8,128)(2,1)} %k_hbm.1, bf16[256,256]{1,0:T(8,128)(2,1)} %v_hbm.1, f32[8,16]{1,0:T(8,128)} %bitcast.3, f32[8,8]{1,0:T(8,128)} %pc_hbm.1), custom_call_target="tpu_custom_call" | custom-call | tf_op jit(solution)/shard_map/pallas_call | solution.py:378
  26.7 0.0 copy-done
  26.7 1.0 %shard_map.65 = bf16[256,1024]{1,0:T(8,128)(2,1)} custom-call(f32[256,1024]{1,0:T(8,128)S(1)} %shard_map.64.attended_ref, f32[1,1024]{1,0:T(1,128)S(1)} %bitcast.2), custom_call_target="tpu_custom_call" | custom-call | tf_op jit(solution)/shard_map/pallas_call | solution.py:411
Async XLA Ops:
  0.0 26.7 %copy-start = (f32[1024]{0:T(1024)S(1)}, f32[1024]{0:T(1024)}, u32[]{:S(2)}) copy-start(f32[1024]{0:T(1024)} %param.11) | copy-start | bytes 12292
where the time goes:
time: 27.8 us; the launch traced here: 27.7 us
  Pallas kernels  27.6 us (99%)
    pallas_call x1, Pallas kernels, local(): pl.pallas_call(functools.partial(kernel, outer_count, inner_count), out_s...  26.7 us
    pallas_call x1, Pallas kernels, local(): pl.pallas_call(norm_kernel, out_shape=jax.ShapeDtypeStruct((tok, HQ * HD)...  0.99 us

commit v1 on v0

v1 whole, which is shorter than its diff:
```python
import contextlib
import functools
import math

import jax
import jax.numpy as jnp
from jax import lax
from jax.experimental import pallas as pl
from jax.experimental.pallas import tpu as pltpu
from jax.sharding import PartitionSpec as P

HQ = 16
KVH = 4
HD = 64
BLOCK = 512
FINE = 16
RATIO = 8
COARSE = 128

EPSILON = 1e-06
LANES = 128
ONES = 16
UNITS = 4
MESH = pl.DeviceIdType.MESH
BF16 = jnp.bfloat16
F32 = jnp.float32
FACTOR = HD ** (-0.5) * math.log2(math.e)


def scope(name):
    return contextlib.nullcontext()


def kernel(
    outer_count, inner_count, use_fine,
    q_hbm, k_hbm, v_hbm, pf_hbm, pc_hbm, out_ref,
    q_ref, k_ref, v_ref, pf_ref, pc_ref, in_sems,
    q_all, queries_t, values_t, own_k, own_v, mate_k, mate_v, other_k, other_v,
    score_ref, weight_ref, peaks, sums, peak_now, decay_next, decay_now,
    fine_send, fine_all, coarse_send, coarse_pad, coarse_all,
    att_send,
    q_ss, q_rs, own_ss, own_rs, mate_ss, mate_rs, other_ss, other_rs,
    fine_ss, fine_rs, cg_ss, cg_rs, co_ss, co_rs, att_ss, att_rs,
):
    tok = q_ref.shape[0]
    ranks = BLOCK // tok
    kv_width = KVH * HD
    share = kv_width // ranks
    q_share = HQ * HD // ranks
    tiles = q_share // LANES
    heads = q_share // HD
    kv_local = share // HD
    heads_kv = heads // kv_local
    fine_dev = tok // FINE
    coarse_dev = tok // COARSE
    group_tok = tok * inner_count
    fine_amount = group_tok // FINE if use_fine else 0
    coarse_group = inner_count * coarse_dev
    coarse_amount = outer_count * coarse_group
    blocks = outer_count * inner_count // ranks
    levels = outer_count.bit_length() - 1

    o_me = lax.axis_index("outer")
    i_me = lax.axis_index("inner")
    linear = o_me * inner_count + i_me
    block = linear // ranks
    rank = lax.rem(linear, ranks)
    odd = lax.rem(block, 2)
    mate = block + 1 - 2 * odd
    relay_from = block - 2 + 4 * odd
    relay_to = block + 2 - 4 * odd
    has_other = (relay_from >= 0) & (relay_from < blocks)
    has_next = (relay_to >= 0) & (relay_to < blocks)

    def at_rank(which_block, rel):
        target_rank = lax.rem(rank + rel, ranks)
        spot = which_block * ranks + target_rank
        return (spot // inner_count, lax.rem(spot, inner_count)), target_rank

    inner_peers = [lax.rem(i_me + rel, inner_count) for rel in range(1, inner_count)]
    outer_peers = [
        o_me + 2 ** level * (1 - 2 * lax.rem(o_me // 2 ** level, 2)) for level in range(levels)]

    loads = [
        pltpu.make_async_copy(src, dst, in_sems.at[n])
        for n, (src, dst) in enumerate((
            (k_hbm, k_ref), (q_hbm, q_ref), (v_hbm, v_ref), (pf_hbm, pf_ref), (pc_hbm, pc_ref)))
    ]
    for load in loads:
        load.start()

    barrier = pltpu.get_barrier_semaphore()

    def greet(device):
        pl.semaphore_signal(barrier, inc=1, device_id=device, device_id_type=MESH)

    for peer in inner_peers:
        greet((o_me, peer))
    for peer in outer_peers:
        greet((peer, i_me))
    for which in (relay_from, relay_to):
        greet(at_rank(lax.rem(which + blocks, blocks), 0)[0])

    def remote(src, dst, send_sem, recv_sem, device):
        return pltpu.make_async_remote_copy(
            src_ref=src, dst_ref=dst, send_sem=send_sem, recv_sem=recv_sem,
            device_id=device, device_id_type=MESH,
        )

    def cols(index, width):
        return pl.ds(pl.multiple_of(index * width, LANES), width)

    def k_at(ref, slot):
        return ref.at[pl.ds(slot * tok, tok)]

    def v_at(ref, slot):
        return ref.at[:, pl.ds(0, HD), pl.ds(slot * tok, tok)]

    own_k_copies, own_q_copies, own_v_copies = [], [], []
    for rel in range(1, ranks):
        device, target = at_rank(block, rel)
        slot = ranks - rel
        own_k_copies.append(remote(
            k_ref.at[:, cols(target, share)], k_at(own_k, slot),
            own_ss.at[0, slot], own_rs.at[0, slot], device))
        own_q_copies.append(remote(
            q_ref.at[:, cols(target, q_share)], q_all.at[slot],
            q_ss.at[slot], q_rs.at[slot], device))
        own_v_copies.append(remote(
            values_t.at[target], v_at(own_v, slot),
            own_ss.at[1, slot], own_rs.at[1, slot], device))
    mate_k_copies, mate_v_copies = [], []
    for rel in range(ranks):
        device, target = at_rank(mate, rel)
        slot = (ranks - rel) % ranks
        mate_k_copies.append(remote(
            k_ref.at[:, cols(target, share)], k_at(mate_k, slot),
            mate_ss.at[0, slot], mate_rs.at[0, slot], device))
        mate_v_copies.append(remote(
            values_t.at[target], v_at(mate_v, slot),
            mate_ss.at[1, slot], mate_rs.at[1, slot], device))
    next_device = at_rank(relay_to, 0)[0]
    relay_k_copies = [remote(
        k_at(mate_k, slot), k_at(other_k, slot),
        other_ss.at[0, slot], other_rs.at[0, slot], next_device) for slot in range(ranks)]
    relay_v_copies = [remote(
        v_at(mate_v, slot), v_at(other_v, slot),
        other_ss.at[1, slot], other_rs.at[1, slot], next_device) for slot in range(ranks)]
    group_copies, fine_copies = [], []
    for n, peer in enumerate(inner_peers):
        peer_rank = lax.rem(peer, ranks)
        group_copies.append(remote(
            coarse_send.at[peer_rank], coarse_pad.at[i_me],
            cg_ss.at[n], cg_rs.at[n], (o_me, peer)))
        if use_fine:
            fine_copies.append(remote(
                fine_send.at[peer_rank], fine_all.at[i_me],
                fine_ss.at[n], fine_rs.at[n], (o_me, peer)))
    outer_copies = []
    for level, peer in enumerate(outer_peers):
        size = 2 ** level
        span = pl.ds(o_me // size * size, size)
        outer_copies.append(remote(
            coarse_all.at[span], coarse_all.at[span], co_ss.at[level], co_rs.at[level],
            (peer, i_me)))

    queries_t[...] = jnp.zeros(queries_t.shape, BF16)
    for ref in (own_v, mate_v, other_v):
        ref[:, HD:, :] = jnp.ones((kv_local, ONES, ref.shape[2]), BF16)

    with scope("wk"):
        loads[0].wait()
    with scope("wbar"):
        pl.semaphore_wait(barrier, inner_count - 1 + levels + 2)
    for copy in own_k_copies + mate_k_copies:
        copy.start()
    with scope("wq"):
        loads[1].wait()
    for copy in own_q_copies:
        copy.start()
    with scope("wv"):
        for load in loads[2:]:
            load.wait()

    def spread(pool):
        rows = pool.shape[0]
        return jnp.concatenate(
            [jnp.broadcast_to(pool[:, n:n + 1], (rows, HD)) for n in range(2 * KVH)], axis=1)

    pf = spread(pf_ref[...].T)
    pc = spread(pc_ref[...])
    paired = jnp.concatenate([k_ref[...], v_ref[...]], axis=1).astype(F32)
    fine = jnp.sum(paired.reshape(fine_dev, FINE, 2 * kv_width) * pf[None], axis=1).astype(BF16)
    fine_wide = fine.astype(F32)
    coarse_wide = jnp.sum(
        fine_wide.reshape(coarse_dev, RATIO, 2 * kv_width) * pc[None], axis=1
    ).astype(BF16).astype(F32)
    padded = coarse_send.shape[1]
    for n in range(ranks):
        k_cols = slice(n * share, (n + 1) * share)
        v_cols = slice(kv_width + n * share, kv_width + (n + 1) * share)
        if use_fine:
            fine_send[n] = jnp.concatenate([fine[:, k_cols], fine[:, v_cols]], axis=1)
        parts = [coarse_wide[:, k_cols], coarse_wide[:, v_cols]]
        if padded > 2 * coarse_dev:
            parts.append(jnp.zeros((padded - 2 * coarse_dev, share), F32))
        coarse_send[n] = jnp.concatenate(parts, axis=0)
    coarse_pad[i_me] = coarse_send[rank]
    if use_fine:
        fine_all[i_me] = fine_send[rank]
    for copy in group_copies:
        copy.start()
    turned = v_ref[...].T
    for n in range(ranks):
        for x in range(kv_local):
            row = n * share + x * HD
            values_t[n, x] = turned[row:row + HD]
    for copy in own_v_copies + mate_v_copies + fine_copies:
        copy.start()

    def arrange(part, tile_of):
        for x in range(tiles):
            turned = tile_of(x).T
            low = (2 * x // heads_kv) * HD
            for y in range(2):
                queries_t[part * heads + 2 * x + y, low:low + HD, :] = turned[y * HD:(y + 1) * HD]

    def score(unit, n, k_set, first):
        amount = k_set.shape[0]
        scores = jnp.dot(k_set, queries_t[unit], preferred_element_type=F32)
        peak = jnp.max(scores, axis=0, keepdims=True)
        if not first:
            before = peaks[unit]
            peak = jnp.maximum(peak, before)
            decay_next[n] = jnp.exp2((before - peak) * FACTOR)
        score_ref[n, 0:amount, :] = scores
        peaks[unit] = peak
        peak_now[n] = peak

    def weigh(n, amount, first):
        weight_ref[n, 0:amount, :] = jnp.exp2(
            (score_ref[n, 0:amount, :] - peak_now[n]) * FACTOR).astype(BF16)
        if not first:
            decay_now[n] = decay_next[n]

    def blend(unit, n, v_set, first):
        amount = v_set.shape[1]
        blended = jnp.dot(v_set, weight_ref[n, 0:amount, :], preferred_element_type=F32)
        sums[unit] = blended if first else sums[unit] * decay_now[n] + blended

    def run(groups, after=None):
        count = len(groups)
        for step in range(count + 2):
            if step >= 2:
                units, _, v_of, amount, first = groups[step - 2]
                for n, unit in enumerate(units):
                    blend(unit, n, v_of(unit % heads // heads_kv), first)
            if 1 <= step < count + 1:
                units, _, _, amount, first = groups[step - 1]
                for n in range(len(units)):
                    weigh(n, amount, first)
            if step < count:
                units, k_of, _, amount, first = groups[step]
                k_set = k_of()
                for n, unit in enumerate(units):
                    score(unit, n, k_set, first)
            if after is not None and step >= 2:
                after(step - 2)

    def units_of(part):
        base = part * heads
        return [list(range(base + n, base + n + UNITS)) for n in range(0, heads, UNITS)]

    def groups_of(parts, k_ref_, v_ref_, span, first):
        amount = span.stop - span.start
        return [
            (units, lambda: k_ref_[span, :], lambda g: v_ref_[g, :, span], amount, first)
            for part in parts for units in units_of(part)]

    with scope("prep0"):
        own_k[0:tok, :] = k_ref[:, cols(rank, share)]
        own_v[:, 0:HD, 0:tok] = values_t[rank]
        arrange(0, lambda x: q_ref[:, cols(rank * tiles + x, LANES)])
    with scope("own0"):
        run(groups_of([0], own_k, own_v, slice(0, tok), True))

    with scope("w_own"):
        for copy in own_k_copies + own_q_copies + own_v_copies:
            copy.wait_recv()
    with scope("prep1"):
        for slot in range(1, ranks):
            arrange(slot, lambda x: q_all[slot, :, x * LANES:(x + 1) * LANES])
    with scope("own1"):
        run(groups_of(range(1, ranks), own_k, own_v, slice(0, BLOCK), True)
            + groups_of([0], own_k, own_v, slice(tok, BLOCK), False))

    with scope("w_group"):
        for copy in group_copies:
            copy.wait_recv()
    for n in range(inner_count):
        rows = slice(n * coarse_dev, (n + 1) * coarse_dev)
        lower = slice(coarse_group + n * coarse_dev, coarse_group + (n + 1) * coarse_dev)
        coarse_all[o_me, rows, :] = coarse_pad[n, 0:coarse_dev, :]
        coarse_all[o_me, lower, :] = coarse_pad[n, coarse_dev:2 * coarse_dev, :]

    def climb(level):
        if level > 0:
            outer_copies[level - 1].wait_recv()
        if level < levels:
            outer_copies[level].start()

    climb(0)
    with scope("w_mk"):
        for copy in mate_k_copies:
            copy.wait_recv()

    @pl.when(has_next)
    def _():
        for copy in relay_k_copies:
            copy.start()

    with scope("climb1"):
        climb(1)
    with scope("w_mv"):
        for copy in mate_v_copies:
            copy.wait_recv()

    @pl.when(has_next)
    def _():
        for copy in relay_v_copies:
            copy.start()

    with scope("climb2"):
        for level in range(2, levels):
            climb(level)
    with scope("mate"):
        run(groups_of(range(ranks), mate_k, mate_v, slice(0, BLOCK), False))

    with scope("climb3"):
        climb(levels)
    with scope("far"):
        far = fine_amount + coarse_amount
        k_far = coarse_all[:, 0:coarse_group, :].reshape(coarse_amount, share)
        v_far = coarse_all[:, coarse_group:, :].reshape(coarse_amount, share)
        if use_fine:
            for copy in fine_copies:
                copy.wait_recv()
            fine_rows = fine_all[...].reshape(fine_amount, 2 * share).astype(F32)
            k_far = jnp.concatenate([fine_rows[:, :share], k_far], axis=0)
            v_far = jnp.concatenate([fine_rows[:, share:], v_far], axis=0)

        def reachable(shape, axis):
            spot = lax.broadcasted_iota(jnp.int32, shape, axis)
            fine_pos = o_me * group_tok + spot * FINE
            coarse_pos = (spot - fine_amount) * COARSE
            position = jnp.where(spot < fine_amount, fine_pos, coarse_pos)
            distance = jnp.abs(lax.div(position, BLOCK) - block)
            outside = (spot < fine_amount) | (lax.div(position, group_tok) != o_me)
            return (distance > 1) & outside

        stand_in = own_k[0:16, :].astype(F32)[0:1, :]
        other_k[BLOCK:, :] = jnp.where(
            reachable((far, share), 0), k_far, jnp.broadcast_to(stand_in, (far, share))).astype(BF16)
        open_cols = reachable((HD, far), 1)
        turned = v_far.T
        for x in range(kv_local):
            other_v[x, 0:HD, BLOCK:] = jnp.where(
                open_cols, turned[x * HD:(x + 1) * HD, :], 0.0).astype(BF16)
            other_v[x, HD:, BLOCK:] = open_cols[0:ONES].astype(F32).astype(BF16)

    @pl.when(has_other)
    def _():
        with scope("w_other"):
            for copy in relay_k_copies + relay_v_copies:
                copy.wait_recv()

    @pl.when(jnp.logical_not(has_other))
    def _():
        other_k[0:BLOCK, :] = own_k[...]
        other_v[:, :, 0:BLOCK] = jnp.zeros((kv_local, HD + ONES, BLOCK), BF16)

    def finish(unit):
        total = sums[unit]
        return total[0:HD] / total[HD:HD + 1]

    def att_copy(part, at):
        device, _ = at_rank(block, part)
        slot = ranks - part - 1
        row = pl.multiple_of(rank * q_share + at * UNITS * HD, HD)
        return remote(att_send.at[part - 1, pl.ds(at * UNITS * HD, UNITS * HD)],
                      out_ref.at[pl.ds(row, UNITS * HD)],
                      att_ss.at[slot, at], att_rs.at[slot, at], device)

    order = list(range(1, ranks)) + [0]
    per_part = heads // UNITS

    def after(index):
        part, at = order[index // per_part], index % per_part
        for n in range(UNITS):
            head = at * UNITS + n
            attended = finish(part * heads + head)
            if part:
                att_send[part - 1, head * HD:(head + 1) * HD, :] = attended
            else:
                out_ref[pl.ds(pl.multiple_of(rank * q_share + head * HD, HD), HD), :] = attended
        if part:
            att_copy(part, at).start()

    with scope("other"):
        run(groups_of(order, other_k, other_v, slice(0, BLOCK + far), False), after)

    with scope("w_att"):
        for part in range(1, ranks):
            for at in range(per_part):
                att_copy(part, at).wait_recv()

    with scope("w_send"):
        for copy in (own_k_copies + own_q_copies + own_v_copies + mate_k_copies + mate_v_copies
                     + group_copies + fine_copies + outer_copies):
            copy.wait_send()

        @pl.when(has_next)
        def _():
            for copy in relay_k_copies + relay_v_copies:
                copy.wait_send()

        for part in range(1, ranks):
            for at in range(per_part):
                att_copy(part, at).wait_send()


def norm_kernel(attended_ref, gain_ref, out_ref):
    attended = attended_ref[...]
    rescale = lax.rsqrt(jnp.mean(attended * attended, axis=0, keepdims=True) + EPSILON)
    out_ref[...] = ((attended * rescale).T * gain_ref[...]).astype(BF16)


def local(outer_count, inner_count, queries, keys, values, pool_fine, pool_coarse, gain):
    tok = queries.shape[0]
    ranks = BLOCK // tok
    share = KVH * HD // ranks
    kv_local = share // HD
    q_share = HQ * HD // ranks
    heads = q_share // HD
    group_tok = tok * inner_count
    use_fine = group_tok > 2 * BLOCK
    far = (group_tok // FINE if use_fine else 0) + outer_count * group_tok // COARSE
    coarse_dev = tok // COARSE
    padded = -(-2 * coarse_dev // 8) * 8
    levels = outer_count.bit_length() - 1
    assert ranks >= 2 and BLOCK % tok == 0 and kv_local == 2 and share == LANES
    assert inner_count % (2 * ranks) == 0 and outer_count == 2 ** levels
    dma = pltpu.SemaphoreType.DMA
    vmem = pltpu.VMEM
    units = ranks * heads
    pair = lambda: dma((2, ranks))
    k_set = lambda amount: vmem((amount, share), BF16)
    v_set = lambda amount: vmem((kv_local, HD + ONES, amount), BF16)
    line = lambda: vmem((UNITS, 1, tok), F32)
    attended = pl.pallas_call(
        functools.partial(kernel, outer_count, inner_count, use_fine),
        out_shape=jax.ShapeDtypeStruct((HQ * HD, tok), F32),
        in_specs=[pl.BlockSpec(memory_space=pltpu.HBM)] * 5,
        out_specs=pl.BlockSpec(memory_space=pltpu.VMEM),
        scratch_shapes=[
            vmem(queries.shape, BF16), vmem(keys.shape, BF16), vmem(values.shape, BF16),
            vmem(pool_fine.shape[::-1], F32), vmem(pool_coarse.shape, F32), dma((5,)),
            vmem((ranks, tok, q_share), BF16),
            vmem((units, share, tok), BF16),
            vmem((ranks, kv_local, HD, tok), BF16),
            k_set(BLOCK), v_set(BLOCK), k_set(BLOCK), v_set(BLOCK),
            k_set(BLOCK + far), v_set(BLOCK + far),
            vmem((UNITS, BLOCK + far, tok), F32),
            vmem((UNITS, BLOCK + far, tok), BF16),
            vmem((units, 1, tok), F32),
            vmem((units, HD + ONES, tok), F32),
            line(), line(), line(),
            vmem((ranks, tok // FINE, 2 * share), BF16),
            vmem((inner_count, tok // FINE, 2 * share), BF16),
            vmem((ranks, padded, share), F32),
            vmem((inner_count, padded, share), F32),
            vmem((outer_count, 2 * inner_count * coarse_dev, share), F32),
            vmem((ranks - 1, q_share, tok), F32),
            dma((ranks,)), dma((ranks,)),
            pair(), pair(), pair(), pair(), pair(), pair(),
            dma((inner_count - 1,)), dma((inner_count - 1,)),
            dma((inner_count - 1,)), dma((inner_count - 1,)),
            dma((levels,)), dma((levels,)),
            dma((ranks - 1, heads // UNITS)), dma((ranks - 1, heads // UNITS)),
        ],
        compiler_params=pltpu.CompilerParams(
            collective_id=0, has_side_effects=True, vmem_limit_bytes=48 * 1024 * 1024),
    )(*(pltpu.with_memory_space_constraint(array, pltpu.HBM) for array in (
        queries, keys, values, pool_fine.T, pool_coarse)))
    return pl.pallas_call(
        norm_kernel,
        out_shape=jax.ShapeDtypeStruct((tok, HQ * HD), BF16),
        in_specs=[pl.BlockSpec(memory_space=pltpu.VMEM)] * 2,
        out_specs=pl.BlockSpec(memory_space=pltpu.VMEM),
        compiler_params=pltpu.CompilerParams(vmem_limit_bytes=8 * 1024 * 1024),
    )(attended, gain.reshape(1, -1))


def solution(mesh):
    rows = P(("outer", "inner"), None)
    return jax.shard_map(
        functools.partial(local, mesh.shape["outer"], mesh.shape["inner"]),
        mesh=mesh, in_specs=(rows, rows, rows, P(), P(), P()),
        out_specs=rows, check_vma=False,
    )
```

time: 27.8 us -> 27 us (0.971)
  the two profiles are of different devices: /device:TPU:9 before, /device:TPU:0 now
where the time goes in v1:
time: 27 us; the launch traced here: 26.9 us
  Pallas kernels  26.8 us (99%)
    pallas_call x1, Pallas kernels, local(): pl.pallas_call(functools.partial(kernel, outer_count, inner_count, use_fi...  25.5 us
    pallas_call x1, Pallas kernels, local(): pl.pallas_call(norm_kernel, out_shape=jax.ShapeDtypeStruct((tok, HQ * HD)...  1.31 us

profile of v1, /device:TPU:0, one launch (start us, length us, event | category | flops | bytes accessed | tf_op | source)
XLA Modules:
  0.0 26.9 jit_solution(3639929538866234131)
XLA Ops:
  0.0 0.0 copy-start
  0.0 25.5 %shard_map.64.attended_ref = f32[1024,256]{1,0:T(8,128)S(1)} custom-call(bf16[256,1024]{1,0:T(8,128)(2,1)} %q_hbm.1, bf16[256,256]{1,0:T(8,128)(2,1)} %k_hbm.1, bf16[256,256]{1,0:T(8,128)(2,1)} %v_hbm.1, f32[8,16]{1,0:T(8,128)} %bitcast.3, f32[8,8]{1,0:T(8,128)} %pc_hbm.1), custom_call_target="tpu_custom_call" | custom-call | tf_op jit(solution)/shard_map/pallas_call | solution.py:460
  25.5 0.0 copy-done
  25.5 1.3 %shard_map.65 = bf16[256,1024]{1,0:T(8,128)(2,1)} custom-call(f32[1024,256]{1,0:T(8,128)S(1)} %shard_map.64.attended_ref, f32[1,1024]{1,0:T(1,128)S(1)} %bitcast.2), custom_call_target="tpu_custom_call" | custom-call | tf_op jit(solution)/shard_map/pallas_call | solution.py:495
Async XLA Ops:
  0.0 25.5 %copy-start = (f32[1024]{0:T(1024)S(1)}, f32[1024]{0:T(1024)}, u32[]{:S(2)}) copy-start(f32[1024]{0:T(1024)} %param.11) | copy-start | bytes 12292

commit v2 on v1

--- a/solution.py
+++ b/solution.py
@@ -98,8 +98,10 @@
         greet((o_me, peer))
     for peer in outer_peers:
         greet((peer, i_me))
-    for which in (relay_from, relay_to):
-        greet(at_rank(lax.rem(which + blocks, blocks), 0)[0])
+    for which, there in ((relay_from, has_other), (relay_to, has_next)):
+        @pl.when(there)
+        def _():
+            greet(at_rank(which, 0)[0])
 
     def remote(src, dst, send_sem, recv_sem, device):
         return pltpu.make_async_remote_copy(
@@ -171,8 +173,9 @@
     with scope("wk"):
         loads[0].wait()
     with scope("wbar"):
-        pl.semaphore_wait(barrier, inner_count - 1 + levels + 2)
-    for copy in own_k_copies + mate_k_copies:
+        pl.semaphore_wait(
+            barrier, inner_count - 1 + levels + has_other.astype(jnp.int32) + has_next.astype(jnp.int32))
+    for copy in own_k_copies + mate_k_copies[:1]:
         copy.start()
     with scope("wq"):
         loads[1].wait()
@@ -208,7 +211,7 @@
     coarse_pad[i_me] = coarse_send[rank]
     if use_fine:
         fine_all[i_me] = fine_send[rank]
-    for copy in group_copies:
+    for copy in group_copies + mate_k_copies[1:]:
         copy.start()
     turned = v_ref[...].T
     for n in range(ranks):
@@ -248,7 +251,7 @@
         blended = jnp.dot(v_set, weight_ref[n, 0:amount, :], preferred_element_type=F32)
         sums[unit] = blended if first else sums[unit] * decay_now[n] + blended
 
-    def run(groups, after=None):
+    def run(groups, after):
         count = len(groups)
         for step in range(count + 2):
             if step >= 2:
@@ -264,8 +267,8 @@
                 k_set = k_of()
                 for n, unit in enumerate(units):
                     score(unit, n, k_set, first)
-            if after is not None and step >= 2:
-                after(step - 2)
+            if step - 2 in after:
+                after[step - 2]()
 
     def units_of(part):
         base = part * heads
@@ -277,12 +280,28 @@
             (units, lambda: k_ref_[span, :], lambda g: v_ref_[g, :, span], amount, first)
             for part in parts for units in units_of(part)]
 
+    def collect():
+        with scope("w_group"):
+            for copy in group_copies:
+                copy.wait_recv()
+        for n in range(inner_count):
+            rows = slice(n * coarse_dev, (n + 1) * coarse_dev)
+            lower = slice(coarse_group + n * coarse_dev, coarse_group + (n + 1) * coarse_dev)
+            coarse_all[o_me, rows, :] = coarse_pad[n, 0:coarse_dev, :]
+            coarse_all[o_me, lower, :] = coarse_pad[n, coarse_dev:2 * coarse_dev, :]
+
+    def climb(level):
+        if level > 0:
+            outer_copies[level - 1].wait_recv()
+        if level < levels:
+            outer_copies[level].start()
+
     with scope("prep0"):
         own_k[0:tok, :] = k_ref[:, cols(rank, share)]
         own_v[:, 0:HD, 0:tok] = values_t[rank]
         arrange(0, lambda x: q_ref[:, cols(rank * tiles + x, LANES)])
     with scope("own0"):
-        run(groups_of([0], own_k, own_v, slice(0, tok), True))
+        run(groups_of([0], own_k, own_v, slice(0, tok), True), {})
 
     with scope("w_own"):
         for copy in own_k_copies + own_q_copies + own_v_copies:
@@ -292,24 +311,9 @@
             arrange(slot, lambda x: q_all[slot, :, x * LANES:(x + 1) * LANES])
     with scope("own1"):
         run(groups_of(range(1, ranks), own_k, own_v, slice(0, BLOCK), True)
-            + groups_of([0], own_k, own_v, slice(tok, BLOCK), False))
-
-    with scope("w_group"):
-        for copy in group_copies:
-            copy.wait_recv()
-    for n in range(inner_count):
-        rows = slice(n * coarse_dev, (n + 1) * coarse_dev)
-        lower = slice(coarse_group + n * coarse_dev, coarse_group + (n + 1) * coarse_dev)
-        coarse_all[o_me, rows, :] = coarse_pad[n, 0:coarse_dev, :]
-        coarse_all[o_me, lower, :] = coarse_pad[n, coarse_dev:2 * coarse_dev, :]
-
-    def climb(level):
-        if level > 0:
-            outer_copies[level - 1].wait_recv()
-        if level < levels:
-            outer_copies[level].start()
-
-    climb(0)
+            + groups_of([0], own_k, own_v, slice(tok, BLOCK), False),
+            {1: lambda: (collect(), climb(0))})
+
     with scope("w_mk"):
         for copy in mate_k_copies:
             copy.wait_recv()
@@ -330,11 +334,9 @@
         for copy in relay_v_copies:
             copy.start()
 
-    with scope("climb2"):
-        for level in range(2, levels):
-            climb(level)
     with scope("mate"):
-        run(groups_of(range(ranks), mate_k, mate_v, slice(0, BLOCK), False))
+        run(groups_of(range(ranks), mate_k, mate_v, slice(0, BLOCK), False),
+            {1: lambda: [climb(level) for level in range(2, levels)]})
 
     with scope("climb3"):
         climb(levels)
@@ -407,7 +409,8 @@
             att_copy(part, at).start()
 
     with scope("other"):
-        run(groups_of(order, other_k, other_v, slice(0, BLOCK + far), False), after)
+        run(groups_of(order, other_k, other_v, slice(0, BLOCK + far), False),
+            {n: functools.partial(after, n) for n in range(ranks * per_part)})
 
     with scope("w_att"):
         for part in range(1, ranks):

time: 27 us -> 23.2 us (0.86)
  Pallas kernels: 26.8 us -> 23 us
    pallas_call x1, Pallas kernels: 25.5 us -> 21.7 us  [local(): pl.pallas_call(functools.partial(kernel, outer_count, inner_count, use_fi...]
where the time goes in v2:
time: 23.2 us; the launch traced here: 23.1 us
  Pallas kernels  23 us (99%)
    pallas_call x1, Pallas kernels, local(): pl.pallas_call(functools.partial(kernel, outer_count, inner_count, use_fi...  21.7 us
    pallas_call x1, Pallas kernels, local(): pl.pallas_call(norm_kernel, out_shape=jax.ShapeDtypeStruct((tok, HQ * HD)...  1.31 us

profile of v2, /device:TPU:0, one launch (start us, length us, event | category | flops | bytes accessed | tf_op | source)
XLA Modules:
  0.0 23.1 jit_solution(1672853909723562028)
XLA Ops:
  0.0 0.0 copy-start
  0.0 21.7 %shard_map.64.attended_ref = f32[1024,256]{1,0:T(8,128)S(1)} custom-call(bf16[256,1024]{1,0:T(8,128)(2,1)} %q_hbm.1, bf16[256,256]{1,0:T(8,128)(2,1)} %k_hbm.1, bf16[256,256]{1,0:T(8,128)(2,1)} %v_hbm.1, f32[8,16]{1,0:T(8,128)} %bitcast.3, f32[8,8]{1,0:T(8,128)} %pc_hbm.1), custom_call_target="tpu_custom_call" | custom-call | tf_op jit(solution)/shard_map/pallas_call | solution.py:463
  21.7 0.0 copy-done
  21.8 1.3 %shard_map.65 = bf16[256,1024]{1,0:T(8,128)(2,1)} custom-call(f32[1024,256]{1,0:T(8,128)S(1)} %shard_map.64.attended_ref, f32[1,1024]{1,0:T(1,128)S(1)} %bitcast.2), custom_call_target="tpu_custom_call" | custom-call | tf_op jit(solution)/shard_map/pallas_call | solution.py:498
Async XLA Ops:
  0.0 21.7 %copy-start = (f32[1024]{0:T(1024)S(1)}, f32[1024]{0:T(1024)}, u32[]{:S(2)}) copy-start(f32[1024]{0:T(1024)} %param.11) | copy-start | bytes 12292

commit v3 on v2

--- a/solution.py
+++ b/solution.py
@@ -33,9 +33,9 @@
 
 def kernel(
     outer_count, inner_count, use_fine,
-    q_hbm, k_hbm, v_hbm, pf_hbm, pc_hbm, out_ref,
+    q_hbm, k_hbm, v_hbm, pf_hbm, pc_hbm, out_ref, got_ref,
     q_ref, k_ref, v_ref, pf_ref, pc_ref, in_sems,
-    q_all, queries_t, values_t, own_k, own_v, mate_k, mate_v, other_k, other_v,
+    q_all, queries_t, values_t, own_k, own_v, mate_k, mate_v, other_k, other_v, far_k, far_v,
     score_ref, weight_ref, peaks, sums, peak_now, decay_next, decay_now,
     fine_send, fine_all, coarse_send, coarse_pad, coarse_all,
     att_send,
@@ -170,19 +170,8 @@
     for ref in (own_v, mate_v, other_v):
         ref[:, HD:, :] = jnp.ones((kv_local, ONES, ref.shape[2]), BF16)
 
-    with scope("wk"):
-        loads[0].wait()
-    with scope("wbar"):
-        pl.semaphore_wait(
-            barrier, inner_count - 1 + levels + has_other.astype(jnp.int32) + has_next.astype(jnp.int32))
-    for copy in own_k_copies + mate_k_copies[:1]:
-        copy.start()
-    with scope("wq"):
-        loads[1].wait()
-    for copy in own_q_copies:
-        copy.start()
-    with scope("wv"):
-        for load in loads[2:]:
+    with scope("wload"):
+        for load in loads:
             load.wait()
 
     def spread(pool):
@@ -211,14 +200,15 @@
     coarse_pad[i_me] = coarse_send[rank]
     if use_fine:
         fine_all[i_me] = fine_send[rank]
-    for copy in group_copies + mate_k_copies[1:]:
-        copy.start()
     turned = v_ref[...].T
     for n in range(ranks):
         for x in range(kv_local):
             row = n * share + x * HD
             values_t[n, x] = turned[row:row + HD]
-    for copy in own_v_copies + mate_v_copies + fine_copies:
+    with scope("wbar"):
+        pl.semaphore_wait(
+            barrier, inner_count - 1 + levels + has_other.astype(jnp.int32) + has_next.astype(jnp.int32))
+    for copy in group_copies + own_k_copies + mate_k_copies[:1] + own_q_copies + own_v_copies:
         copy.start()
 
     def arrange(part, tile_of):
@@ -240,35 +230,35 @@
         peaks[unit] = peak
         peak_now[n] = peak
 
-    def weigh(n, amount, first):
-        weight_ref[n, 0:amount, :] = jnp.exp2(
+    def weigh(unit, n, amount, first):
+        weight_ref[unit, 0:amount, :] = jnp.exp2(
             (score_ref[n, 0:amount, :] - peak_now[n]) * FACTOR).astype(BF16)
         if not first:
-            decay_now[n] = decay_next[n]
-
-    def blend(unit, n, v_set, first):
+            decay_now[unit] = decay_next[n]
+
+    def blend(unit, v_set, first):
         amount = v_set.shape[1]
-        blended = jnp.dot(v_set, weight_ref[n, 0:amount, :], preferred_element_type=F32)
-        sums[unit] = blended if first else sums[unit] * decay_now[n] + blended
-
-    def run(groups, after):
+        blended = jnp.dot(v_set, weight_ref[unit, 0:amount, :], preferred_element_type=F32)
+        sums[unit] = blended if first else sums[unit] * decay_now[unit] + blended
+
+    def run(groups, lag, hooks):
         count = len(groups)
-        for step in range(count + 2):
-            if step >= 2:
-                units, _, v_of, amount, first = groups[step - 2]
-                for n, unit in enumerate(units):
-                    blend(unit, n, v_of(unit % heads // heads_kv), first)
+        for step in range(count + lag):
+            if step >= lag:
+                units, _, v_of, amount, first = groups[step - lag]
+                for unit in units:
+                    blend(unit, v_of(unit % heads // heads_kv), first)
             if 1 <= step < count + 1:
                 units, _, _, amount, first = groups[step - 1]
-                for n in range(len(units)):
-                    weigh(n, amount, first)
+                for n, unit in enumerate(units):
+                    weigh(unit, n, amount, first)
             if step < count:
                 units, k_of, _, amount, first = groups[step]
                 k_set = k_of()
                 for n, unit in enumerate(units):
                     score(unit, n, k_set, first)
-            if step - 2 in after:
-                after[step - 2]()
+            if step in hooks:
+                hooks[step]()
 
     def units_of(part):
         base = part * heads
@@ -301,42 +291,66 @@
         own_v[:, 0:HD, 0:tok] = values_t[rank]
         arrange(0, lambda x: q_ref[:, cols(rank * tiles + x, LANES)])
     with scope("own0"):
-        run(groups_of([0], own_k, own_v, slice(0, tok), True), {})
+        run(groups_of([0], own_k, own_v, slice(0, tok), True), 2, {})
+    for copy in mate_k_copies[1:]:
+        copy.start()
 
     with scope("w_own"):
         for copy in own_k_copies + own_q_copies + own_v_copies:
             copy.wait_recv()
+    for copy in mate_v_copies[:1]:
+        copy.start()
     with scope("prep1"):
         for slot in range(1, ranks):
             arrange(slot, lambda x: q_all[slot, :, x * LANES:(x + 1) * LANES])
+
+    def start_all(copies):
+        for copy in copies:
+            copy.start()
+
+    def relay(name, arrivals, onward):
+        with scope(name):
+            for copy in arrivals:
+                copy.wait_recv()
+
+        @pl.when(has_next)
+        def _():
+            start_all(onward)
+
     with scope("own1"):
         run(groups_of(range(1, ranks), own_k, own_v, slice(0, BLOCK), True)
-            + groups_of([0], own_k, own_v, slice(tok, BLOCK), False),
-            {1: lambda: (collect(), climb(0))})
-
-    with scope("w_mk"):
-        for copy in mate_k_copies:
-            copy.wait_recv()
-
-    @pl.when(has_next)
-    def _():
-        for copy in relay_k_copies:
-            copy.start()
-
+            + groups_of([0], own_k, own_v, slice(tok, BLOCK), False), 2,
+            {0: lambda: start_all(mate_v_copies[1:] + fine_copies),
+             2: lambda: (collect(), climb(0)),
+             4: lambda: relay("w_mk0", mate_k_copies[:1], relay_k_copies[:1])})
+
+    relay("w_mk1", mate_k_copies[1:], relay_k_copies[1:])
     with scope("climb1"):
         climb(1)
-    with scope("w_mv"):
-        for copy in mate_v_copies:
-            copy.wait_recv()
-
-    @pl.when(has_next)
+    mate_groups = groups_of(range(ranks), mate_k, mate_v, slice(0, BLOCK), False)
+    with scope("mate"):
+        run(mate_groups, len(mate_groups) + 1, {
+            1: lambda: relay("w_mv0", mate_v_copies[:1], relay_v_copies[:1]),
+            len(mate_groups): lambda: relay("w_mv1", mate_v_copies[1:], relay_v_copies[1:])})
+    with scope("climb2"):
+        for level in range(2, levels):
+            climb(level)
+
+    @pl.when(has_other)
     def _():
-        for copy in relay_v_copies:
-            copy.start()
-
-    with scope("mate"):
-        run(groups_of(range(ranks), mate_k, mate_v, slice(0, BLOCK), False),
-            {1: lambda: [climb(level) for level in range(2, levels)]})
+        with scope("w_other"):
+            for copy in relay_k_copies:
+                copy.wait_recv()
+
+        def arrive():
+            with scope("w_otherv"):
+                for copy in relay_v_copies:
+                    copy.wait_recv()
+
+        other_groups = groups_of(range(ranks), other_k, other_v, slice(0, BLOCK), False)
+        count = len(other_groups)
+        with scope("other"):
+            run(other_groups, count + 1, {count: arrive})
 
     with scope("climb3"):
         climb(levels)
@@ -361,25 +375,14 @@
             return (distance > 1) & outside
 
         stand_in = own_k[0:16, :].astype(F32)[0:1, :]
-        other_k[BLOCK:, :] = jnp.where(
+        far_k[...] = jnp.where(
             reachable((far, share), 0), k_far, jnp.broadcast_to(stand_in, (far, share))).astype(BF16)
         open_cols = reachable((HD, far), 1)
         turned = v_far.T
         for x in range(kv_local):
-            other_v[x, 0:HD, BLOCK:] = jnp.where(
+            far_v[x, 0:HD, :] = jnp.where(
                 open_cols, turned[x * HD:(x + 1) * HD, :], 0.0).astype(BF16)
-            other_v[x, HD:, BLOCK:] = open_cols[0:ONES].astype(F32).astype(BF16)
-
-    @pl.when(has_other)
-    def _():
-        with scope("w_other"):
-            for copy in relay_k_copies + relay_v_copies:
-                copy.wait_recv()
-
-    @pl.when(jnp.logical_not(has_other))
-    def _():
-        other_k[0:BLOCK, :] = own_k[...]
-        other_v[:, :, 0:BLOCK] = jnp.zeros((kv_local, HD + ONES, BLOCK), BF16)
+            far_v[x, HD:, :] = open_cols[0:ONES].astype(F32).astype(BF16)
 
     def finish(unit):
         total = sums[unit]
@@ -388,9 +391,8 @@
     def att_copy(part, at):
         device, _ = at_rank(block, part)
         slot = ranks - part - 1
-        row = pl.multiple_of(rank * q_share + at * UNITS * HD, HD)
-        return remote(att_send.at[part - 1, pl.ds(at * UNITS * HD, UNITS * HD)],
-                      out_ref.at[pl.ds(row, UNITS * HD)],
+        span = pl.ds(at * UNITS * HD, UNITS * HD)
+        return remote(att_send.at[part - 1, span], got_ref.at[slot, span],
                       att_ss.at[slot, at], att_rs.at[slot, at], device)
 
     order = list(range(1, ranks)) + [0]
@@ -402,15 +404,15 @@
             head = at * UNITS + n
             attended = finish(part * heads + head)
             if part:
-                att_send[part - 1, head * HD:(head + 1) * HD, :] = attended
+                att_send[part - 1, head * HD:(head + 1) * HD, :] = attended.astype(BF16)
             else:
-                out_ref[pl.ds(pl.multiple_of(rank * q_share + head * HD, HD), HD), :] = attended
+                out_ref[head * HD:(head + 1) * HD, :] = attended
         if part:
             att_copy(part, at).start()
 
-    with scope("other"):
-        run(groups_of(order, other_k, other_v, slice(0, BLOCK + far), False),
-            {n: functools.partial(after, n) for n in range(ranks * per_part)})
+    far_groups = groups_of(order, far_k, far_v, slice(0, far), False)
+    with scope("farrun"):
+        run(far_groups, 2, {2 + n: functools.partial(after, n) for n in range(len(far_groups))})
 
     with scope("w_att"):
         for part in range(1, ranks):
@@ -432,10 +434,17 @@
                 att_copy(part, at).wait_send()
 
 
-def norm_kernel(attended_ref, gain_ref, out_ref):
-    attended = attended_ref[...]
-    rescale = lax.rsqrt(jnp.mean(attended * attended, axis=0, keepdims=True) + EPSILON)
-    out_ref[...] = ((attended * rescale).T * gain_ref[...]).astype(BF16)
+def norm_kernel(kept_ref, got_ref, gain_ref, out_ref):
+    parts = got_ref.shape[0] + 1
+    width = kept_ref.shape[0]
+    rank = lax.rem(lax.axis_index("inner"), parts)
+    blocks = [kept_ref[...]] + [got_ref[n].astype(F32) for n in range(parts - 1)]
+    total = sum(jnp.sum(x * x, axis=0, keepdims=True) for x in blocks)
+    rescale = lax.rsqrt(total / (parts * width) + EPSILON)
+    for n, x in enumerate(blocks):
+        column = lax.rem(rank + n, parts)
+        cols = pl.ds(pl.multiple_of(column * width, LANES), width)
+        out_ref[:, cols] = ((x * rescale).T * gain_ref[:, cols]).astype(BF16)
 
 
 def local(outer_count, inner_count, queries, keys, values, pool_fine, pool_coarse, gain):
@@ -460,11 +469,12 @@
     k_set = lambda amount: vmem((amount, share), BF16)
     v_set = lambda amount: vmem((kv_local, HD + ONES, amount), BF16)
     line = lambda: vmem((UNITS, 1, tok), F32)
-    attended = pl.pallas_call(
+    kept, got = pl.pallas_call(
         functools.partial(kernel, outer_count, inner_count, use_fine),
-        out_shape=jax.ShapeDtypeStruct((HQ * HD, tok), F32),
+        out_shape=[jax.ShapeDtypeStruct((q_share, tok), F32),
+                   jax.ShapeDtypeStruct((ranks - 1, q_share, tok), BF16)],
         in_specs=[pl.BlockSpec(memory_space=pltpu.HBM)] * 5,
-        out_specs=pl.BlockSpec(memory_space=pltpu.VMEM),
+        out_specs=[pl.BlockSpec(memory_space=pltpu.VMEM)] * 2,
         scratch_shapes=[
             vmem(queries.shape, BF16), vmem(keys.shape, BF16), vmem(values.shape, BF16),
             vmem(pool_fine.shape[::-1], F32), vmem(pool_coarse.shape, F32), dma((5,)),
@@ -472,18 +482,18 @@
             vmem((units, share, tok), BF16),
             vmem((ranks, kv_local, HD, tok), BF16),
             k_set(BLOCK), v_set(BLOCK), k_set(BLOCK), v_set(BLOCK),
-            k_set(BLOCK + far), v_set(BLOCK + far),
-            vmem((UNITS, BLOCK + far, tok), F32),
-            vmem((UNITS, BLOCK + far, tok), BF16),
+            k_set(BLOCK), v_set(BLOCK), k_set(far), v_set(far),
+            vmem((UNITS, max(BLOCK, far), tok), F32),
+            vmem((units, max(BLOCK, far), tok), BF16),
             vmem((units, 1, tok), F32),
             vmem((units, HD + ONES, tok), F32),
-            line(), line(), line(),
+            line(), line(), vmem((units, 1, tok), F32),
             vmem((ranks, tok // FINE, 2 * share), BF16),
             vmem((inner_count, tok // FINE, 2 * share), BF16),
             vmem((ranks, padded, share), F32),
             vmem((inner_count, padded, share), F32),
             vmem((outer_count, 2 * inner_count * coarse_dev, share), F32),
-            vmem((ranks - 1, q_share, tok), F32),
+            vmem((ranks - 1, q_share, tok), BF16),
             dma((ranks,)), dma((ranks,)),
             pair(), pair(), pair(), pair(), pair(), pair(),
             dma((inner_count - 1,)), dma((inner_count - 1,)),
@@ -498,10 +508,10 @@
     return pl.pallas_call(
         norm_kernel,
         out_shape=jax.ShapeDtypeStruct((tok, HQ * HD), BF16),
-        in_specs=[pl.BlockSpec(memory_space=pltpu.VMEM)] * 2,
+        in_specs=[pl.BlockSpec(memory_space=pltpu.VMEM)] * 3,
         out_specs=pl.BlockSpec(memory_space=pltpu.VMEM),
         compiler_params=pltpu.CompilerParams(vmem_limit_bytes=8 * 1024 * 1024),
-    )(attended, gain.reshape(1, -1))
+    )(kept, got, gain.reshape(1, -1))
 
 
 def solution(mesh):

time: 23.2 us -> 21.2 us (0.914)
  the two profiles are of different devices: /device:TPU:0 before, /device:TPU:17 now
where the time goes in v3:
time: 21.2 us; the launch traced here: 21 us
  Pallas kernels  21 us (99%)
    pallas_call x1, Pallas kernels, local(): pl.pallas_call(functools.partial(kernel, outer_count, inner_count, use_fi...  19.7 us
    pallas_call x1, Pallas kernels, local(): pl.pallas_call(norm_kernel, out_shape=jax.ShapeDtypeStruct((tok, HQ * HD)...  1.27 us

profile of v3, /device:TPU:17, one launch (start us, length us, event | category | flops | bytes accessed | tf_op | source)
XLA Modules:
  0.0 21.0 jit_solution(15524778884283990614)
XLA Ops:
  0.0 0.0 copy-start
  0.0 19.7 %shard_map.64 = (f32[512,256]{1,0:T(8,128)S(1)}, bf16[1,512,256]{2,1,0:T(8,128)(2,1)S(1)}) custom-call(bf16[256,1024]{1,0:T(8,128)(2,1)} %q_hbm.1, bf16[256,256]{1,0:T(8,128)(2,1)} %k_hbm.1, bf16[256,256]{1,0:T(8,128)(2,1)} %v_hbm.1, f32[8,16]{1,0:T(8,128)} %bitcast.3, f32[8,8]{1,0:T(8,128)} %pc_hbm.1), custom_call_target="tpu_custom_call" | custom-call | tf_op jit(solution)/shard_map/pallas_call | solution.py:472
  19.7 0.0 copy-done
  19.7 1.3 %shard_map.65 = bf16[256,1024]{1,0:T(8,128)(2,1)} custom-call(f32[512,256]{1,0:T(8,128)S(1)} %get-tuple-element.7.kept_ref, bf16[1,512,256]{2,1,0:T(8,128)(2,1)S(1)} %get-tuple-element.8.got_ref, f32[1,1024]{1,0:T(1,128)S(1)} %bitcast.2), custom_call_target="tpu_custom_call" | custom-call | tf_op jit(solution)/shard_map/pallas_call | solution.py:508
Async XLA Ops:
  0.0 19.7 %copy-start = (f32[1024]{0:T(1024)S(1)}, f32[1024]{0:T(1024)}, u32[]{:S(2)}) copy-start(f32[1024]{0:T(1024)} %param.11) | copy-start | bytes 12292

commit v4 on v3

--- a/solution.py
+++ b/solution.py
@@ -36,11 +36,11 @@
     q_hbm, k_hbm, v_hbm, pf_hbm, pc_hbm, out_ref, got_ref,
     q_ref, k_ref, v_ref, pf_ref, pc_ref, in_sems,
     q_all, queries_t, values_t, own_k, own_v, mate_k, mate_v, other_k, other_v, far_k, far_v,
-    score_ref, weight_ref, peaks, sums, peak_now, decay_next, decay_now,
+    score_ref, weight_ref, peaks, sums, peak_now, decay_next, decay_now, far_weights, far_decays,
     fine_send, fine_all, coarse_send, coarse_pad, coarse_all,
     att_send,
     q_ss, q_rs, own_ss, own_rs, mate_ss, mate_rs, other_ss, other_rs,
-    fine_ss, fine_rs, cg_ss, cg_rs, co_ss, co_rs, att_ss, att_rs,
+    fine_ss, fine_rs, cg_ss, cg_rs, co_ss, co_rs, att_ss, att_rs, token_sems,
 ):
     tok = q_ref.shape[0]
     ranks = BLOCK // tok
@@ -58,7 +58,7 @@
     coarse_group = inner_count * coarse_dev
     coarse_amount = outer_count * coarse_group
     blocks = outer_count * inner_count // ranks
-    levels = outer_count.bit_length() - 1
+    turns = outer_count // 2 - 1
 
     o_me = lax.axis_index("outer")
     i_me = lax.axis_index("inner")
@@ -78,8 +78,7 @@
         return (spot // inner_count, lax.rem(spot, inner_count)), target_rank
 
     inner_peers = [lax.rem(i_me + rel, inner_count) for rel in range(1, inner_count)]
-    outer_peers = [
-        o_me + 2 ** level * (1 - 2 * lax.rem(o_me // 2 ** level, 2)) for level in range(levels)]
+    outer_peers = [lax.rem(o_me + rel, outer_count) for rel in range(1, outer_count)]
 
     loads = [
         pltpu.make_async_copy(src, dst, in_sems.at[n])
@@ -96,12 +95,17 @@
 
     for peer in inner_peers:
         greet((o_me, peer))
-    for peer in outer_peers:
-        greet((peer, i_me))
-    for which, there in ((relay_from, has_other), (relay_to, has_next)):
+    greet((o_me + 1 - 2 * lax.rem(o_me, 2), i_me))
+    line = ((o_me - 2, o_me >= 2), (o_me + 2, o_me + 2 < outer_count))
+    near = [((o, i_me), there) for o, there in line]
+    near += [(at_rank(which, 0)[0], there)
+             for which, there in ((relay_from, has_other), (relay_to, has_next))]
+    for device, there in near:
         @pl.when(there)
         def _():
-            greet(at_rank(which, 0)[0])
+            greet(device)
+    line_count = sum(there.astype(jnp.int32) for _, there in line)
+    near_count = sum(there.astype(jnp.int32) for _, there in near)
 
     def remote(src, dst, send_sem, recv_sem, device):
         return pltpu.make_async_remote_copy(
@@ -158,13 +162,9 @@
             fine_copies.append(remote(
                 fine_send.at[peer_rank], fine_all.at[i_me],
                 fine_ss.at[n], fine_rs.at[n], (o_me, peer)))
-    outer_copies = []
-    for level, peer in enumerate(outer_peers):
-        size = 2 ** level
-        span = pl.ds(o_me // size * size, size)
-        outer_copies.append(remote(
-            coarse_all.at[span], coarse_all.at[span], co_ss.at[level], co_rs.at[level],
-            (peer, i_me)))
+    outer_copies = [remote(
+        coarse_all.at[o_me], coarse_all.at[o_me], co_ss.at[n], co_rs.at[n], (peer, i_me))
+        for n, peer in enumerate(outer_peers)]
 
     queries_t[...] = jnp.zeros(queries_t.shape, BF16)
     for ref in (own_v, mate_v, other_v):
@@ -207,9 +207,38 @@
             values_t[n, x] = turned[row:row + HD]
     with scope("wbar"):
         pl.semaphore_wait(
-            barrier, inner_count - 1 + levels + has_other.astype(jnp.int32) + has_next.astype(jnp.int32))
-    for copy in group_copies + own_k_copies + mate_k_copies[:1] + own_q_copies + own_v_copies:
+            barrier, inner_count + near_count)
+
+    def pass_on(turn):
+        for o, there in line:
+            @pl.when(there)
+            def _():
+                pl.semaphore_signal(
+                    token_sems.at[turn], inc=1, device_id=(o, i_me), device_id_type=MESH)
+
+    def hear(turn):
+        if turn < turns:
+            with scope("tok%d" % turn):
+                pl.semaphore_wait(token_sems.at[turn], line_count)
+        if turn + 1 < turns:
+            pass_on(turn + 1)
+
+    for copy in group_copies:
         copy.start()
+    own_copies = own_k_copies + own_q_copies + own_v_copies
+
+    @pl.when(rank == 0)
+    def _():
+        for copy in own_copies + mate_k_copies[:1]:
+            copy.start()
+
+    @pl.when(rank > 0)
+    def _():
+        for copy in mate_k_copies[:1] + own_copies:
+            copy.start()
+
+    if turns > 0:
+        pass_on(0)
 
     def arrange(part, tile_of):
         for x in range(tiles):
@@ -230,28 +259,31 @@
         peaks[unit] = peak
         peak_now[n] = peak
 
-    def weigh(unit, n, amount, first):
-        weight_ref[unit, 0:amount, :] = jnp.exp2(
+    def weigh(unit, n, amount, first, weights=weight_ref, decays=decay_now):
+        weights[unit, 0:amount, :] = jnp.exp2(
             (score_ref[n, 0:amount, :] - peak_now[n]) * FACTOR).astype(BF16)
         if not first:
-            decay_now[unit] = decay_next[n]
+            decays[unit] = decay_next[n]
+
+    def product(unit, v_set, weights):
+        return jnp.dot(
+            v_set, weights[unit, 0:v_set.shape[1], :], preferred_element_type=F32)
 
     def blend(unit, v_set, first):
-        amount = v_set.shape[1]
-        blended = jnp.dot(v_set, weight_ref[unit, 0:amount, :], preferred_element_type=F32)
+        blended = product(unit, v_set, weight_ref)
         sums[unit] = blended if first else sums[unit] * decay_now[unit] + blended
 
-    def run(groups, lag, hooks):
+    def run(groups, lag, hooks, *into):
         count = len(groups)
-        for step in range(count + lag):
-            if step >= lag:
+        for step in range(count + (1 if lag is None else lag)):
+            if lag is not None and step >= lag:
                 units, _, v_of, amount, first = groups[step - lag]
                 for unit in units:
                     blend(unit, v_of(unit % heads // heads_kv), first)
             if 1 <= step < count + 1:
                 units, _, _, amount, first = groups[step - 1]
                 for n, unit in enumerate(units):
-                    weigh(unit, n, amount, first)
+                    weigh(unit, n, amount, first, *into)
             if step < count:
                 units, k_of, _, amount, first = groups[step]
                 k_set = k_of()
@@ -280,11 +312,15 @@
             coarse_all[o_me, rows, :] = coarse_pad[n, 0:coarse_dev, :]
             coarse_all[o_me, lower, :] = coarse_pad[n, coarse_dev:2 * coarse_dev, :]
 
-    def climb(level):
-        if level > 0:
-            outer_copies[level - 1].wait_recv()
-        if level < levels:
-            outer_copies[level].start()
+    def share_coarse():
+        collect()
+        for turn in range(2, turns):
+            hear(turn)
+        start_all(outer_copies)
+
+    def start_all(copies):
+        for copy in copies:
+            copy.start()
 
     with scope("prep0"):
         own_k[0:tok, :] = k_ref[:, cols(rank, share)]
@@ -294,6 +330,7 @@
         run(groups_of([0], own_k, own_v, slice(0, tok), True), 2, {})
     for copy in mate_k_copies[1:]:
         copy.start()
+    hear(0)
 
     with scope("w_own"):
         for copy in own_k_copies + own_q_copies + own_v_copies:
@@ -304,10 +341,6 @@
         for slot in range(1, ranks):
             arrange(slot, lambda x: q_all[slot, :, x * LANES:(x + 1) * LANES])
 
-    def start_all(copies):
-        for copy in copies:
-            copy.start()
-
     def relay(name, arrivals, onward):
         with scope(name):
             for copy in arrivals:
@@ -321,39 +354,29 @@
         run(groups_of(range(1, ranks), own_k, own_v, slice(0, BLOCK), True)
             + groups_of([0], own_k, own_v, slice(tok, BLOCK), False), 2,
             {0: lambda: start_all(mate_v_copies[1:] + fine_copies),
-             2: lambda: (collect(), climb(0)),
-             4: lambda: relay("w_mk0", mate_k_copies[:1], relay_k_copies[:1])})
+             1: lambda: hear(1),
+             3: share_coarse,
+             5: lambda: relay("w_mk0", mate_k_copies[:1], relay_k_copies[:1])})
 
     relay("w_mk1", mate_k_copies[1:], relay_k_copies[1:])
-    with scope("climb1"):
-        climb(1)
+    order = list(range(1, ranks)) + [0]
     mate_groups = groups_of(range(ranks), mate_k, mate_v, slice(0, BLOCK), False)
     with scope("mate"):
         run(mate_groups, len(mate_groups) + 1, {
-            1: lambda: relay("w_mv0", mate_v_copies[:1], relay_v_copies[:1]),
-            len(mate_groups): lambda: relay("w_mv1", mate_v_copies[1:], relay_v_copies[1:])})
-    with scope("climb2"):
-        for level in range(2, levels):
-            climb(level)
-
+            len(mate_groups) - 2: lambda: relay("w_mv0", mate_v_copies[:1], relay_v_copies[:1]),
+            len(mate_groups) - 1: lambda: relay("w_mv1", mate_v_copies[1:], relay_v_copies[1:])})
     @pl.when(has_other)
     def _():
         with scope("w_other"):
             for copy in relay_k_copies:
                 copy.wait_recv()
 
-        def arrive():
-            with scope("w_otherv"):
-                for copy in relay_v_copies:
-                    copy.wait_recv()
-
-        other_groups = groups_of(range(ranks), other_k, other_v, slice(0, BLOCK), False)
-        count = len(other_groups)
         with scope("other"):
-            run(other_groups, count + 1, {count: arrive})
-
-    with scope("climb3"):
-        climb(levels)
+            run(groups_of(order, other_k, other_v, slice(0, BLOCK), False), None, {})
+
+    with scope("w_outer"):
+        for copy in outer_copies:
+            copy.wait_recv()
     with scope("far"):
         far = fine_amount + coarse_amount
         k_far = coarse_all[:, 0:coarse_group, :].reshape(coarse_amount, share)
@@ -384,10 +407,6 @@
                 open_cols, turned[x * HD:(x + 1) * HD, :], 0.0).astype(BF16)
             far_v[x, HD:, :] = open_cols[0:ONES].astype(F32).astype(BF16)
 
-    def finish(unit):
-        total = sums[unit]
-        return total[0:HD] / total[HD:HD + 1]
-
     def att_copy(part, at):
         device, _ = at_rank(block, part)
         slot = ranks - part - 1
@@ -395,24 +414,41 @@
         return remote(att_send.at[part - 1, span], got_ref.at[slot, span],
                       att_ss.at[slot, at], att_rs.at[slot, at], device)
 
-    order = list(range(1, ranks)) + [0]
     per_part = heads // UNITS
-
-    def after(index):
-        part, at = order[index // per_part], index % per_part
-        for n in range(UNITS):
-            head = at * UNITS + n
-            attended = finish(part * heads + head)
-            if part:
-                att_send[part - 1, head * HD:(head + 1) * HD, :] = attended.astype(BF16)
-            else:
-                out_ref[head * HD:(head + 1) * HD, :] = attended
-        if part:
-            att_copy(part, at).start()
-
-    far_groups = groups_of(order, far_k, far_v, slice(0, far), False)
     with scope("farrun"):
-        run(far_groups, 2, {2 + n: functools.partial(after, n) for n in range(len(far_groups))})
+        run(groups_of(order, far_k, far_v, slice(0, far), False), None, {}, far_weights, far_decays)
+
+    def finish(with_other):
+        for part in order:
+            for at in range(per_part):
+                for head in range(at * UNITS, (at + 1) * UNITS):
+                    unit = part * heads + head
+                    g = head // heads_kv
+                    total = sums[unit]
+                    if with_other:
+                        total = total * decay_now[unit] + product(unit, other_v[g], weight_ref)
+                    total = total * far_decays[unit] + product(unit, far_v[g], far_weights)
+                    attended = total[0:HD] / total[HD:HD + 1]
+                    rows = slice(head * HD, (head + 1) * HD)
+                    if part:
+                        att_send[part - 1, rows, :] = attended.astype(BF16)
+                    else:
+                        out_ref[rows, :] = attended
+                if part:
+                    att_copy(part, at).start()
+
+    @pl.when(has_other)
+    def _():
+        with scope("w_otherv"):
+            for copy in relay_v_copies:
+                copy.wait_recv()
+        with scope("fin"):
+            finish(True)
+
+    @pl.when(jnp.logical_not(has_other))
+    def _():
+        with scope("fin"):
+            finish(False)
 
     with scope("w_att"):
         for part in range(1, ranks):
@@ -459,9 +495,8 @@
     far = (group_tok // FINE if use_fine else 0) + outer_count * group_tok // COARSE
     coarse_dev = tok // COARSE
     padded = -(-2 * coarse_dev // 8) * 8
-    levels = outer_count.bit_length() - 1
     assert ranks >= 2 and BLOCK % tok == 0 and kv_local == 2 and share == LANES
-    assert inner_count % (2 * ranks) == 0 and outer_count == 2 ** levels
+    assert inner_count % (2 * ranks) == 0 and outer_count % 2 == 0
     dma = pltpu.SemaphoreType.DMA
     vmem = pltpu.VMEM
     units = ranks * heads
@@ -484,10 +519,11 @@
             k_set(BLOCK), v_set(BLOCK), k_set(BLOCK), v_set(BLOCK),
             k_set(BLOCK), v_set(BLOCK), k_set(far), v_set(far),
             vmem((UNITS, max(BLOCK, far), tok), F32),
-            vmem((units, max(BLOCK, far), tok), BF16),
+            vmem((units, BLOCK, tok), BF16),
             vmem((units, 1, tok), F32),
             vmem((units, HD + ONES, tok), F32),
             line(), line(), vmem((units, 1, tok), F32),
+            vmem((units, far, tok), BF16), vmem((units, 1, tok), F32),
             vmem((ranks, tok // FINE, 2 * share), BF16),
             vmem((inner_count, tok // FINE, 2 * share), BF16),
             vmem((ranks, padded, share), F32),
@@ -498,8 +534,9 @@
             pair(), pair(), pair(), pair(), pair(), pair(),
             dma((inner_count - 1,)), dma((inner_count - 1,)),
             dma((inner_count - 1,)), dma((inner_count - 1,)),
-            dma((levels,)), dma((levels,)),
+            dma((outer_count - 1,)), dma((outer_count - 1,)),
             dma((ranks - 1, heads // UNITS)), dma((ranks - 1, heads // UNITS)),
+            pltpu.SemaphoreType.REGULAR((max(outer_count // 2 - 1, 1),)),
         ],
         compiler_params=pltpu.CompilerParams(
             collective_id=0, has_side_effects=True, vmem_limit_bytes=48 * 1024 * 1024),

time: 21.2 us -> 19.5 us (0.920)
  the two profiles are of different devices: /device:TPU:17 before, /device:TPU:5 now
where the time goes in v4:
time: 19.5 us; the launch traced here: 19.3 us
  Pallas kernels  19.3 us (99%)
    pallas_call x1, Pallas kernels, local(): pl.pallas_call(functools.partial(kernel, outer_count, inner_count, use_fi...  18.1 us
    pallas_call x1, Pallas kernels, local(): pl.pallas_call(norm_kernel, out_shape=jax.ShapeDtypeStruct((tok, HQ * HD)...  1.27 us

profile of v4, /device:TPU:5, one launch (start us, length us, event | category | flops | bytes accessed | tf_op | source)
XLA Modules:
  0.0 19.3 jit_solution(16159255440827866889)
XLA Ops:
  0.0 0.0 copy-start
  0.0 18.1 %shard_map.64 = (f32[512,256]{1,0:T(8,128)S(1)}, bf16[1,512,256]{2,1,0:T(8,128)(2,1)S(1)}) custom-call(bf16[256,1024]{1,0:T(8,128)(2,1)} %q_hbm.1, bf16[256,256]{1,0:T(8,128)(2,1)} %k_hbm.1, bf16[256,256]{1,0:T(8,128)(2,1)} %v_hbm.1, f32[8,16]{1,0:T(8,128)} %bitcast.3, f32[8,8]{1,0:T(8,128)} %pc_hbm.1), custom_call_target="tpu_custom_call" | custom-call | tf_op jit(solution)/shard_map/pallas_call | solution.py:507
  18.1 0.0 copy-done
  18.1 1.3 %shard_map.65 = bf16[256,1024]{1,0:T(8,128)(2,1)} custom-call(f32[512,256]{1,0:T(8,128)S(1)} %get-tuple-element.7.kept_ref, bf16[1,512,256]{2,1,0:T(8,128)(2,1)S(1)} %get-tuple-element.8.got_ref, f32[1,1024]{1,0:T(1,128)S(1)} %bitcast.2), custom_call_target="tpu_custom_call" | custom-call | tf_op jit(solution)/shard_map/pallas_call | solution.py:545
Async XLA Ops:
  0.0 18.1 %copy-start = (f32[1024]{0:T(1024)S(1)}, f32[1024]{0:T(1024)}, u32[]{:S(2)}) copy-start(f32[1024]{0:T(1024)} %param.11) | copy-start | bytes 12292
